TPU v7x, 256 devices: a whole 4x4x8 slice. The times are simulated.
256 devices in a mesh: dp: 16 (over x_hi, z), param: 16 (over y, x_lo, core).
Axes of the slice: x: 4 (x_hi: 2, x_lo: 2; x = x_hi * 2 + x_lo), y: 4, z: 8, core: 2. Of those that a mesh axis runs over, the one named last changes fastest.
Arguments:
- ex_grads: bfloat16 [1536, 20480], P('dp', 'param'), may hold values from -6 to 6
- tgt_grads: bfloat16 [4096, 20480], P('dp', 'param'), may hold values from -6 to 6
- projection: bfloat16 [20480, 4096], P('param'), may hold values from -0.0390625 to 0.0390625
- example_weight: float32 [1536], P('param'), may hold values from 0.05 to 1
Outputs:
- scores: float32 [4096, 1536], P('dp', 'param')
All inputs are finite; a program needn't handle non-finite values.
Results may differ from a plain program's by a relative error of at most 0.0078.
Values may be sent and summed in bfloat16 or wider, within the bound.
A program may use at most 192 MiB of HBM per device.

v0:
```python
import math
import jax
import jax.numpy as jnp
from jax import lax
from jax.sharding import PartitionSpec as P

ridge_value = 0.5


def sent_to_all(x, axis):
    length = lax.axis_size(axis)
    return lax.all_to_all(jnp.broadcast_to(x[None], (length, *x.shape)), axis, 0, 0, tiled=True)


def in_order(parts, dim):
    parts = jnp.moveaxis(parts, 0, dim)
    lengths = parts.shape
    return parts.reshape(*lengths[:dim], lengths[dim] * lengths[dim + 1], *lengths[dim + 2 :])


def gather_directly(x, axis, dim):
    parts = sent_to_all(x, axis)
    return in_order(parts, dim)


def with_ridge(block, first_row):
    row_ids = lax.broadcasted_iota(jnp.int32, block.shape, 0) + first_row
    col_ids = lax.broadcasted_iota(jnp.int32, block.shape, 1)
    return block + jnp.where(row_ids == col_ids, ridge_value, 0.0).astype(jnp.float32)


def on_device(ex_grads, tgt_grads, projection, example_weight):
    ex_rows = ex_grads.shape[0]
    columns = projection.shape[1]
    param_total = lax.axis_size("param")
    param_pos = lax.axis_index("param")
    replica_pos = lax.axis_index("dp")
    stacked = jnp.concatenate([ex_grads, tgt_grads], axis=0)
    contract_rows = (((0,), (1,)), ((), ()))
    feature_block = lax.psum_scatter(
        lax.dot_general(projection, stacked, contract_rows, preferred_element_type=jnp.float32),
        "param",
        scatter_dimension=0,
        tiled=True,
    )
    local_features = feature_block.astype(jnp.bfloat16)
    example_part = local_features[:, :ex_rows]
    contract_first = (((0,), (0,)), ((), ()))
    partial_value = lax.dot_general(
        local_features,
        gather_directly(example_part, "dp", 1),
        contract_first,
        preferred_element_type=jnp.float32,
    )
    examples = partial_value.shape[1]
    summed = lax.psum(partial_value, "param")
    kernel_block = with_ridge(summed[:ex_rows] / columns, replica_pos * ex_rows)
    kernel = lax.all_gather(kernel_block, "dp", axis=0, tiled=True)
    cross_terms = summed[ex_rows:] / columns
    factor = jnp.linalg.cholesky(kernel)
    forward = jax.scipy.linalg.solve_triangular(factor, cross_terms.T, lower=True)
    solved = jax.scipy.linalg.solve_triangular(factor, forward, lower=True, trans=1)
    block_cols = examples // param_total
    chosen = lax.dynamic_slice_in_dim(solved.T, param_pos * block_cols, block_cols, 1)
    return chosen * math.sqrt(columns) * example_weight[None, :]


def solution(mesh):
    placed = (P("dp", "param"), P("dp", "param"), P("param", None), P("param"))
    return jax.shard_map(
        on_device, mesh=mesh, in_specs=placed, out_specs=P("dp", "param"), check_vma=False
    )
```

profile of v0, /device:TPU:1, one launch (start us, length us, event | category | flops | bytes accessed | tf_op | source)
XLA Modules:
  0.0 965.1 jit_solution(2935307158991540555)
XLA Ops:
  6.5 10.7 %convolution_bitcast_fusion = f32[4096,352]{0,1:T(8,128)} fusion(bf16[1280,4096]{1,0:T(8,128)(2,1)} %param.6, bf16[256,1280]{1,0:T(8,128)(2,1)} %param.5, bf16[96,1280]{1,0:T(8,128)(2,1)} %param.4), kind=kOutput, calls=%fused_computation.6 | convolution fusion | flops 3692789760 | bytes 17154048 | tf_op jit(solution)/shard_map/dot_general | solution.py:41
  17.3 79.7 %reduce-scatter.2.cloned.1.call-done = f32[256,352]{0,1:T(8,128)} async-done(((f32[4096,352]{0,1:T(8,128)}), f32[256,352]{0,1:T(8,128)}) %reduce-scatter.2.cloned.1.call-update) | async-done | bytes 360464 | tf_op jit(solution)/shard_map/reduce_scatter | solution.py:40
  98.1 27.1 %all_to_all.5 = bf16[16,256,96]{1,2,0:T(8,128)(2,1)S(1)} all-to-all(bf16[16,256,96]{1,2,0:T(8,128)(2,1)S(1)} %broadcast_in_dim.17), channel_id=1, replica_groups=mesh['dp'=16,'param'=16] {'dp'}, dimensions={0} | all-to-all | bytes 1572864 | tf_op jit(solution)/shard_map/all_to_all | solution.py:12
  127.1 130.4 %all-reduce.3.cloned.1.call-done = f32[352,1536]{1,0:T(8,128)} async-done(((f32[352,1536]{1,0:T(8,128)}), f32[352,1536]{1,0:T(8,128)}) %all-reduce.3.cloned.1.call-update) | async-done | bytes 2162704 | tf_op jit(solution)/shard_map/psum | solution.py:56
  261.1 144.9 %all-gather.2.cloned.1.call-done = f32[1536,1536]{1,0:T(8,128)} async-done(((f32[96,1536]{1,0:T(8,128)}), f32[1536,1536]{1,0:T(8,128)}) %all-gather.2.cloned.1.call-update) | async-done | bytes 9437200 | tf_op jit(solution)/shard_map/all_gather | solution.py:58
  406.0 10.1 %copy.10 = f32[1536,1536]{0,1:T(8,128)} copy(f32[1536,1536]{1,0:T(8,128)} %all-gather.2.cloned.1.call-done) | data formatting | bytes 18874368 | tf_op jit(solution)/shard_map/all_gather | solution.py:58
  416.1 12.3 %fusion = f32[1536,1536]{1,0:T(8,128)} fusion(f32[1536,1536]{1,0:T(8,128)} %all-gather.2.cloned.1.call-done, f32[1536,1536]{0,1:T(8,128)} %copy.10), kind=kLoop, calls=%fused_computation.4 | loop fusion | flops 4718592 | bytes 28311552 | tf_op jit(solution)/shard_map/jit(cholesky)/div | solution.py:60
  429.3 11.7 %cholesky.341 = f32[128,128]{1,0:T(8,128)S(1)} custom-call(f32[128,128]{1,0:T(8,128)S(1)} %cholesky.892), custom_call_target="Cholesky" | custom-call | tf_op jit(solution)/shard_map/jit(cholesky)/cholesky | solution.py:60
  445.8 9.8 %custom-call.98 = f32[1,128,128]{1,2,0:T(8,128)S(1)} custom-call(f32[1,128,128]{2,1,0:T(8,128)S(1)} %get-tuple-element.111), custom_call_target="InvertDiagBlocksLowerTriangular" | custom-call | tf_op jit(solution)/shard_map/jit(cholesky)/cholesky | solution.py:60
  460.3 11.9 %cholesky.362 = f32[128,128]{1,0:T(8,128)S(1)} custom-call(f32[128,128]{1,0:T(8,128)S(1)} %cholesky.896), custom_call_target="Cholesky" | custom-call | tf_op jit(solution)/shard_map/jit(cholesky)/cholesky | solution.py:60
  472.9 9.8 %custom-call.99 = f32[1,128,128]{1,2,0:T(8,128)S(1)} custom-call(f32[1,128,128]{2,1,0:T(8,128)S(1)} %get-tuple-element.108), custom_call_target="InvertDiagBlocksLowerTriangular" | custom-call | tf_op jit(solution)/shard_map/jit(cholesky)/cholesky | solution.py:60
  487.0 11.7 %cholesky.385 = f32[128,128]{1,0:T(8,128)S(1)} custom-call(f32[128,128]{1,0:T(8,128)S(1)} %cholesky.901), custom_call_target="Cholesky" | custom-call | tf_op jit(solution)/shard_map/jit(cholesky)/cholesky | solution.py:60
  499.4 10.0 %custom-call.100 = f32[1,128,128]{1,2,0:T(8,128)S(1)} custom-call(f32[1,128,128]{2,1,0:T(8,128)S(1)} %get-tuple-element.105), custom_call_target="InvertDiagBlocksLowerTriangular" | custom-call | tf_op jit(solution)/shard_map/jit(cholesky)/cholesky | solution.py:60
  514.3 11.7 %cholesky.715 = f32[128,128]{1,0:T(8,128)S(1)} custom-call(f32[128,128]{1,0:T(8,128)S(1)} %cholesky.906), custom_call_target="Cholesky" | custom-call | tf_op jit(solution)/shard_map/jit(cholesky)/cholesky | solution.py:60
  526.6 9.8 %custom-call.101 = f32[1,128,128]{1,2,0:T(8,128)S(1)} custom-call(f32[1,128,128]{2,1,0:T(8,128)S(1)} %get-tuple-element.102), custom_call_target="InvertDiagBlocksLowerTriangular" | custom-call | tf_op jit(solution)/shard_map/jit(cholesky)/cholesky | solution.py:60
  541.4 12.1 %cholesky.734 = f32[128,128]{1,0:T(8,128)S(1)} custom-call(f32[128,128]{1,0:T(8,128)S(1)} %cholesky.911), custom_call_target="Cholesky" | custom-call | tf_op jit(solution)/shard_map/jit(cholesky)/cholesky | solution.py:60
  554.2 9.8 %custom-call.102 = f32[1,128,128]{1,2,0:T(8,128)S(1)} custom-call(f32[1,128,128]{2,1,0:T(8,128)S(1)} %get-tuple-element.99), custom_call_target="InvertDiagBlocksLowerTriangular" | custom-call | tf_op jit(solution)/shard_map/jit(cholesky)/cholesky | solution.py:60
  569.1 11.7 %cholesky.754 = f32[128,128]{1,0:T(8,128)S(1)} custom-call(f32[128,128]{1,0:T(8,128)S(1)} %cholesky.916), custom_call_target="Cholesky" | custom-call | tf_op jit(solution)/shard_map/jit(cholesky)/cholesky | solution.py:60
  581.5 10.0 %custom-call.103 = f32[1,128,128]{1,2,0:T(8,128)S(1)} custom-call(f32[1,128,128]{2,1,0:T(8,128)S(1)} %get-tuple-element.96), custom_call_target="InvertDiagBlocksLowerTriangular" | custom-call | tf_op jit(solution)/shard_map/jit(cholesky)/cholesky | solution.py:60
  596.6 11.7 %cholesky.774 = f32[128,128]{1,0:T(8,128)S(1)} custom-call(f32[128,128]{1,0:T(8,128)S(1)} %cholesky.921), custom_call_target="Cholesky" | custom-call | tf_op jit(solution)/shard_map/jit(cholesky)/cholesky | solution.py:60
  609.0 9.8 %custom-call.104 = f32[1,128,128]{1,2,0:T(8,128)S(1)} custom-call(f32[1,128,128]{2,1,0:T(8,128)S(1)} %get-tuple-element.93), custom_call_target="InvertDiagBlocksLowerTriangular" | custom-call | tf_op jit(solution)/shard_map/jit(cholesky)/cholesky | solution.py:60
  624.1 11.7 %cholesky.794 = f32[128,128]{1,0:T(8,128)S(1)} custom-call(f32[128,128]{1,0:T(8,128)S(1)} %cholesky.926), custom_call_target="Cholesky" | custom-call | tf_op jit(solution)/shard_map/jit(cholesky)/cholesky | solution.py:60
  636.5 9.8 %custom-call.105 = f32[1,128,128]{1,2,0:T(8,128)S(1)} custom-call(f32[1,128,128]{2,1,0:T(8,128)S(1)} %get-tuple-element.90), custom_call_target="InvertDiagBlocksLowerTriangular" | custom-call | tf_op jit(solution)/shard_map/jit(cholesky)/cholesky | solution.py:60
  650.9 12.2 %cholesky.814 = f32[128,128]{1,0:T(8,128)S(1)} custom-call(f32[128,128]{1,0:T(8,128)S(1)} %cholesky.931), custom_call_target="Cholesky" | custom-call | tf_op jit(solution)/shard_map/jit(cholesky)/cholesky | solution.py:60
  663.7 9.8 %custom-call.106 = f32[1,128,128]{1,2,0:T(8,128)S(1)} custom-call(f32[1,128,128]{2,1,0:T(8,128)S(1)} %get-tuple-element.87), custom_call_target="InvertDiagBlocksLowerTriangular" | custom-call | tf_op jit(solution)/shard_map/jit(cholesky)/cholesky | solution.py:60
  677.9 11.7 %cholesky.834 = f32[128,128]{1,0:T(8,128)S(1)} custom-call(f32[128,128]{1,0:T(8,128)S(1)} %cholesky.936), custom_call_target="Cholesky" | custom-call | tf_op jit(solution)/shard_map/jit(cholesky)/cholesky | solution.py:60
  690.2 9.8 %custom-call.107 = f32[1,128,128]{1,2,0:T(8,128)S(1)} custom-call(f32[1,128,128]{2,1,0:T(8,128)S(1)} %get-tuple-element.84), custom_call_target="InvertDiagBlocksLowerTriangular" | custom-call | tf_op jit(solution)/shard_map/jit(cholesky)/cholesky | solution.py:60
  703.7 11.9 %cholesky.854 = f32[128,128]{1,0:T(8,128)S(1)} custom-call(f32[128,128]{1,0:T(8,128)S(1)} %cholesky.941), custom_call_target="Cholesky" | custom-call | tf_op jit(solution)/shard_map/jit(cholesky)/cholesky | solution.py:60
  716.2 9.8 %custom-call.108 = f32[1,128,128]{1,2,0:T(8,128)S(1)} custom-call(f32[1,128,128]{2,1,0:T(8,128)S(1)} %get-tuple-element.81), custom_call_target="InvertDiagBlocksLowerTriangular" | custom-call | tf_op jit(solution)/shard_map/jit(cholesky)/cholesky | solution.py:60
  729.2 11.7 %cholesky.872 = f32[128,128]{1,0:T(8,128)S(1)} custom-call(f32[128,128]{1,0:T(8,128)S(1)} %convolution_subtract_fusion.25), custom_call_target="Cholesky" | custom-call | tf_op jit(solution)/shard_map/jit(cholesky)/cholesky | solution.py:60
  765.2 35.2 %while.1 = (s32[]{:T(128)}, f32[1536,1536]{1,0:T(8,128)}, s32[12,2]{0,1:T(2,128)S(1)}, f32[12,128,128]{2,1,0:T(8,128)S(1)}, s32[]{:T(128)}) while((s32[]{:T(128)}, f32[1536,1536]{1,0:T(8,128)}, s32[12,2]{0,1:T(2,128)S(1)}, f32[12,128,128]{2,1,0:T(8,128)S(1)}, s32[]{:T(128)}) %tuple.106), condition=%wide.while_cond, body=%wide.while_body.sunk | while | flops 2 | bytes 131189 | solution.py:62
  800.4 118.3 %custom-call.109 = f32[12,128,128]{1,2,0:T(8,128)S(1)} custom-call(f32[12,128,128]{2,1,0:T(8,128)S(1)} %get-tuple-element.12), custom_call_target="InvertDiagBlocksLowerTriangular" | custom-call | tf_op jit(solution)/shard_map/jit(_solve_triangular)/triangular_solve | solution.py:62
  (222 shorter events, 159.5 us)
Async XLA Ops:
  6.5 90.4 %reduce-scatter.2.cloned.1.call-start = ((), (), s32[]{:S(2)}) async-start(), calls=%async_computation.2 | async-start | bytes 6127616 | tf_op jit(solution)/shard_map/reduce_scatter | solution.py:40
  17.2 240.3 %all-reduce.3.cloned.1.call-start = ((), (), s32[]{:S(2)}) async-start(), calls=%async_computation.3 | async-start | bytes 4325376 | tf_op jit(solution)/shard_map/psum | solution.py:56
  127.0 132.5 %copy-start.1 = (f32[96]{0:T(128)S(1)}, f32[96]{0:T(128)}, u32[]{:S(2)}) copy-start(f32[96]{0:T(128)} %param.7) | copy-start | bytes 1156
  127.1 278.9 %all-gather.2.cloned.1.call-start = ((), (), s32[]{:S(2)}) async-start(), calls=%async_computation.4 | async-start | bytes 10027008 | tf_op jit(solution)/shard_map/all_gather | solution.py:58
  920.3 9.7 %copy-start = (f32[1536,1536]{1,0:T(8,128)S(1)}, f32[1536,1536]{1,0:T(8,128)}, u32[]{:S(2)}) copy-start(f32[1536,1536]{1,0:T(8,128)} %get-tuple-element.190) | copy-start | bytes 28311556
Sparse Core Ops, SparseCore 0:
  17.4 79.5 reduce-scatter.1
  127.2 130.2 all-reduce.2
  260.1 145.8 all-gather.1
where the time goes:
time: 970 us; the launch traced here: 965 us
  other arithmetic  409 us (42%)
  waiting for transfers between devices  355 us (37%)
  matrix products  100 us (10%)
  local copies, waits for them, and re-layouts  51.6 us (5%)
  blocking collectives  27.1 us (3%)
  between operations  22.1 us (2%)
    another operation x46, other arithmetic, on_device(): factor = jnp.linalg.cholesky(kernel)  265 us
    all_gather x1, waiting for transfers between devices, on_device(): kernel = lax.all_gather(kernel_block, 'dp', axis=0, tiled=True)  145 us
    psum x1, waiting for transfers between devices, on_device(): summed = lax.psum(partial_value, 'param')  130 us
    another operation x3, other arithmetic, on_device(): jax.scipy.linalg.solve_triangular(factor, forward, lower=True, trans=1)  127 us
    reduce_scatter x1, waiting for transfers between devices, on_device(): lax.psum_scatter(lax.dot_general(projection, stacked, contract_rows, pref...  79.7 us
    another operation x22, matrix products, on_device(): factor = jnp.linalg.cholesky(kernel)  50.1 us
    another operation x36, local copies, waits for them, and re-layouts  35 us
    all_to_all x1, blocking collectives, sent_to_all(): lax.all_to_all(jnp.broadcast_to(x[None], (length, *x.shape)), axis, 0, 0,...  27.1 us
  transfers between devices with their start and end apart: 3, of which 3 were waited for; matrix products, arithmetic and copies ran while one was open for 0% of the time, Pallas kernels for 0%

commit v1 on v0

--- a/solution.py
+++ b/solution.py
@@ -53,7 +53,7 @@
         preferred_element_type=jnp.float32,
     )
     examples = partial_value.shape[1]
-    summed = lax.psum(partial_value, "param")
+    summed = jnp.sum(lax.all_gather(partial_value, "param"), axis=0)
     kernel_block = with_ridge(summed[:ex_rows] / columns, replica_pos * ex_rows)
     kernel = lax.all_gather(kernel_block, "dp", axis=0, tiled=True)
     cross_terms = summed[ex_rows:] / columns

time: 970 us -> 1030 us (1.062)
  waiting for transfers between devices: 355 us -> 401 us
  other arithmetic: 409 us -> 420 us
  local copies, waits for them, and re-layouts: 51.6 us -> 62.5 us
    all_gather x0 -> x1, waiting for transfers between devices: none -> 179 us  [on_device(): summed = jnp.sum(lax.all_gather(partial_value, 'param'), axis=0)]
    psum x1 -> x0, waiting for transfers between devices: 130 us -> none  [on_device(): summed = lax.psum(partial_value, 'param')]
    reduce_sum x0 -> x1, other arithmetic: none -> 12.2 us  [on_device(): summed = jnp.sum(lax.all_gather(partial_value, 'param'), axis=0)]
where the time goes in v1:
time: 1030 us; the launch traced here: 1020 us
  other arithmetic  420 us (41%)
  waiting for transfers between devices  401 us (39%)
  matrix products  90.6 us (9%)
  local copies, waits for them, and re-layouts  62.5 us (6%)
  blocking collectives  26.7 us (3%)
  between operations  22.3 us (2%)
    another operation x46, other arithmetic, on_device(): factor = jnp.linalg.cholesky(kernel)  265 us
    all_gather x1, waiting for transfers between devices, on_device(): summed = jnp.sum(lax.all_gather(partial_value, 'param'), axis=0)  179 us
    all_gather x1, waiting for transfers between devices, on_device(): kernel = lax.all_gather(kernel_block, 'dp', axis=0, tiled=True)  142 us
    another operation x3, other arithmetic, on_device(): jax.scipy.linalg.solve_triangular(factor, forward, lower=True, trans=1)  127 us
    reduce_scatter x1, waiting for transfers between devices, on_device(): lax.psum_scatter(lax.dot_general(projection, stacked, contract_rows, pref...  79.7 us
    another operation x22, matrix products, on_device(): factor = jnp.linalg.cholesky(kernel)  50.3 us
    another operation x36, local copies, waits for them, and re-layouts  42.9 us
    all_to_all x1, blocking collectives, sent_to_all(): lax.all_to_all(jnp.broadcast_to(x[None], (length, *x.shape)), axis, 0, 0,...  26.7 us
  transfers between devices with their start and end apart: 3, of which 3 were waited for; matrix products, arithmetic and copies ran while one was open for 0% of the time, Pallas kernels for 0%

profile of v1, /device:TPU:1, one launch (start us, length us, event | category | flops | bytes accessed | tf_op | source)
XLA Modules:
  0.0 1022.5 jit_solution(11903064251099431684)
XLA Ops:
  6.5 10.7 %convolution_bitcast_fusion = f32[4096,352]{0,1:T(8,128)} fusion(bf16[1280,4096]{1,0:T(8,128)(2,1)} %param.6, bf16[256,1280]{1,0:T(8,128)(2,1)} %param.5, bf16[96,1280]{1,0:T(8,128)(2,1)} %param.4), kind=kOutput, calls=%fused_computation.6 | convolution fusion | flops 3692789760 | bytes 17154048 | tf_op jit(solution)/shard_map/dot_general | solution.py:41
  17.3 79.7 %reduce-scatter.2.cloned.1.call-done = f32[256,352]{0,1:T(8,128)} async-done(((f32[4096,352]{0,1:T(8,128)}), f32[256,352]{0,1:T(8,128)}) %reduce-scatter.2.cloned.1.call-update) | async-done | bytes 360464 | tf_op jit(solution)/shard_map/reduce_scatter | solution.py:40
  98.1 26.7 %all_to_all.5 = bf16[16,256,96]{1,2,0:T(8,128)(2,1)S(1)} all-to-all(bf16[16,256,96]{1,2,0:T(8,128)(2,1)S(1)} %broadcast_in_dim.17), channel_id=1, replica_groups=mesh['dp'=16,'param'=16] {'dp'}, dimensions={0} | all-to-all | bytes 1572864 | tf_op jit(solution)/shard_map/all_to_all | solution.py:12
  126.7 178.8 %all-gather.6.cloned.1.call-done = f32[5632,1536]{1,0:T(8,128)} async-done(((f32[352,1536]{1,0:T(8,128)}), f32[5632,1536]{1,0:T(8,128)}) %all-gather.6.cloned.1.call-update) | async-done | bytes 34603024 | tf_op jit(solution)/shard_map/all_gather | solution.py:56
  305.5 12.2 %reduce_sum.9 = f32[352,1536]{1,0:T(8,128)S(1)} reduce(f32[16,352,1536]{2,1,0:T(8,128)} %bitcast.208, f32[]{:T(128)} %constant.418.clone.1), dimensions={0}, to_apply=%region_1.0 | reduce | flops 8110080 | bytes 36765700 | tf_op jit(solution)/shard_map/reduce_sum | solution.py:56
  322.0 142.4 %all-gather.4.cloned.1.call-done = f32[1536,1536]{1,0:T(8,128)} async-done(((f32[96,1536]{1,0:T(8,128)}), f32[1536,1536]{1,0:T(8,128)}) %all-gather.4.cloned.1.call-update) | async-done | bytes 9437200 | tf_op jit(solution)/shard_map/all_gather | solution.py:58
  464.3 9.9 copy.8
  474.2 12.6 %fusion = f32[1536,1536]{1,0:T(8,128)} fusion(f32[1536,1536]{1,0:T(8,128)} %all-gather.4.cloned.1.call-done, f32[1536,1536]{0,1:T(8,128)} %copy.8), kind=kLoop, calls=%fused_computation.4 | loop fusion | flops 4718592 | bytes 28311552 | tf_op jit(solution)/shard_map/jit(cholesky)/div | solution.py:60
  487.6 11.7 %cholesky.341 = f32[128,128]{1,0:T(8,128)S(1)} custom-call(f32[128,128]{1,0:T(8,128)S(1)} %cholesky.892), custom_call_target="Cholesky" | custom-call | tf_op jit(solution)/shard_map/jit(cholesky)/cholesky | solution.py:60
  504.2 9.8 custom-call.98
  518.7 12.1 %cholesky.362 = f32[128,128]{1,0:T(8,128)S(1)} custom-call(f32[128,128]{1,0:T(8,128)S(1)} %cholesky.896), custom_call_target="Cholesky" | custom-call | tf_op jit(solution)/shard_map/jit(cholesky)/cholesky | solution.py:60
  531.4 9.8 custom-call.99
  545.6 11.7 %cholesky.385 = f32[128,128]{1,0:T(8,128)S(1)} custom-call(f32[128,128]{1,0:T(8,128)S(1)} %cholesky.901), custom_call_target="Cholesky" | custom-call | tf_op jit(solution)/shard_map/jit(cholesky)/cholesky | solution.py:60
  558.7 10.0 custom-call.100
  573.5 11.7 %cholesky.715 = f32[128,128]{1,0:T(8,128)S(1)} custom-call(f32[128,128]{1,0:T(8,128)S(1)} %cholesky.906), custom_call_target="Cholesky" | custom-call | tf_op jit(solution)/shard_map/jit(cholesky)/cholesky | solution.py:60
  586.5 9.8 custom-call.101
  601.5 11.9 %cholesky.734 = f32[128,128]{1,0:T(8,128)S(1)} custom-call(f32[128,128]{1,0:T(8,128)S(1)} %cholesky.911), custom_call_target="Cholesky" | custom-call | tf_op jit(solution)/shard_map/jit(cholesky)/cholesky | solution.py:60
  614.7 9.8 custom-call.102
  629.7 11.7 %cholesky.754 = f32[128,128]{1,0:T(8,128)S(1)} custom-call(f32[128,128]{1,0:T(8,128)S(1)} %cholesky.916), custom_call_target="Cholesky" | custom-call | tf_op jit(solution)/shard_map/jit(cholesky)/cholesky | solution.py:60
  642.8 10.2 custom-call.103
  658.1 11.7 %cholesky.774 = f32[128,128]{1,0:T(8,128)S(1)} custom-call(f32[128,128]{1,0:T(8,128)S(1)} %cholesky.921), custom_call_target="Cholesky" | custom-call | tf_op jit(solution)/shard_map/jit(cholesky)/cholesky | solution.py:60
  671.1 9.8 custom-call.104
  686.1 11.7 %cholesky.794 = f32[128,128]{1,0:T(8,128)S(1)} custom-call(f32[128,128]{1,0:T(8,128)S(1)} %cholesky.926), custom_call_target="Cholesky" | custom-call | tf_op jit(solution)/shard_map/jit(cholesky)/cholesky | solution.py:60
  699.1 9.8 custom-call.105
  713.6 12.1 %cholesky.814 = f32[128,128]{1,0:T(8,128)S(1)} custom-call(f32[128,128]{1,0:T(8,128)S(1)} %cholesky.931), custom_call_target="Cholesky" | custom-call | tf_op jit(solution)/shard_map/jit(cholesky)/cholesky | solution.py:60
  727.0 9.8 custom-call.106
  741.2 11.7 %cholesky.834 = f32[128,128]{1,0:T(8,128)S(1)} custom-call(f32[128,128]{1,0:T(8,128)S(1)} %cholesky.936), custom_call_target="Cholesky" | custom-call | tf_op jit(solution)/shard_map/jit(cholesky)/cholesky | solution.py:60
  754.2 9.8 custom-call.107
  767.8 11.9 %cholesky.854 = f32[128,128]{1,0:T(8,128)S(1)} custom-call(f32[128,128]{1,0:T(8,128)S(1)} %cholesky.941), custom_call_target="Cholesky" | custom-call | tf_op jit(solution)/shard_map/jit(cholesky)/cholesky | solution.py:60
  793.9 11.7 %cholesky.872 = f32[128,128]{1,0:T(8,128)S(1)} custom-call(f32[128,128]{1,0:T(8,128)S(1)} %convolution_subtract_fusion.25), custom_call_target="Cholesky" | custom-call | tf_op jit(solution)/shard_map/jit(cholesky)/cholesky | solution.py:60
  823.7 42.9 %while.1 = (s32[]{:T(128)}, f32[1536,1536]{1,0:T(8,128)}, s32[12,2]{0,1:T(2,128)S(1)}, f32[12,128,128]{2,1,0:T(8,128)}, s32[]{:T(128)}) while((s32[]{:T(128)}, f32[1536,1536]{1,0:T(8,128)}, s32[12,2]{0,1:T(2,128)S(1)}, f32[12,128,128]{2,1,0:T(8,128)}, s32[]{:T(128)}) %tuple.106), condition=%wide.while_cond, body=%wide.while_body.sunk | while | flops 2 | bytes 132705 | solution.py:62
  866.6 118.9 %custom-call.109 = f32[12,128,128]{1,2,0:T(8,128)S(1)} custom-call(f32[12,128,128]{2,1,0:T(8,128)} %get-tuple-element.12), custom_call_target="InvertDiagBlocksLowerTriangular" | custom-call | tf_op jit(solution)/shard_map/jit(_solve_triangular)/triangular_solve | solution.py:62
  (225 shorter events, 168.3 us)
Async XLA Ops:
  6.5 90.4 %reduce-scatter.2.cloned.1.call-start = ((), (), s32[]{:S(2)}) async-start(), calls=%async_computation.2 | async-start | bytes 6127616 | tf_op jit(solution)/shard_map/reduce_scatter | solution.py:40
  17.2 288.2 %all-gather.6.cloned.1.call-start = ((), (), s32[]{:S(2)}) async-start(), calls=%async_computation.4 | async-start | bytes 36765696 | tf_op jit(solution)/shard_map/all_gather | solution.py:56
  126.6 337.7 %all-gather.4.cloned.1.call-start = ((), (), s32[]{:S(2)}) async-start(), calls=%async_computation.3 | async-start | bytes 10027008 | tf_op jit(solution)/shard_map/all_gather | solution.py:58
  317.6 1.0 copy-start.1
  986.9 7.9 copy-start
Sparse Core Ops, SparseCore 0:
  17.4 79.5 reduce-scatter.1
  126.7 178.6 all-gather.5
  318.8 145.5 all-gather.3
